TPU v7x, 32 devices: a whole 2x2x4 slice. The times are simulated.
32 devices in a mesh: shard: 8 (over y, x, core), dp: 4 (over z).
Axes of the slice: x: 2, y: 2, z: 4, core: 2. Of those that a mesh axis runs over, the one named last changes fastest.
Arguments:
- grad: float32 [288, 128, 4096], P('shard', 'dp'), may hold values from -252 to 252
- param: bfloat16 [288, 128, 4096], P('shard', 'dp'), may hold values from -0.119628906 to 0.119628906
- row_state: float32 [288, 128], P('shard', 'dp'), may hold values from 0.3 to 27
- col_state: float32 [3, 4096], replicated, may hold values from 0.002 to 400
- block_start: int32 [8], replicated, may hold values from 0 to 143, as said below
- block_matrix: int32 [144], replicated, may hold values from 0 to 2, as said below
- step: int32 [1], replicated, may hold values from 2 to 11
Outputs:
- new_params: bfloat16 [18432, 4096], P(None, 'shard')
- new_row_state: float32 [288, 128], P('shard', 'dp')
- new_col_state: float32 [3, 4096], replicated
Inputs may be any that keep to these rules, and one draw needn't show every extreme that they name: block_start rises from 0 at index 0; every shard index owns between 1 and 36 consecutive global blocks, held in its first slots, and some index owns exactly 36; slots past a device's owned count hold values that no output reads. `block_matrix`: ids 0 and 1 each label 4096 / 128 blocks and id 2 labels 10240 / 128 blocks, in any order.
All inputs are finite; a program needn't handle non-finite values.
Results may differ from a plain program's by a relative error of at most 0.0004.
Values may be sent and summed in bfloat16 or wider, within the bound.
A program may use at most 192 MiB of HBM per device.

v0:
```python
import jax
import jax.numpy as jnp
from jax import lax
from jax.sharding import PartitionSpec as P

D = 4096
FF = 10240


def scale_grad(grad, safe_rows, matrix_pick, new_cols, row_avg):
    slot_cols = jnp.dot(matrix_pick, new_cols, precision=lax.Precision.HIGHEST)
    slot_avg = jnp.dot(matrix_pick, row_avg, precision=lax.Precision.HIGHEST)
    return grad / jnp.sqrt(safe_rows[:, :, None] * slot_cols[:, None, :] / slot_avg[:, None, None])


def body(grad, param, row_state, col_state, block_start, block_matrix, step):
    slot_count = grad.shape[0]
    total_blocks = block_matrix.shape[0]
    shard_index = lax.axis_index("shard")
    block_ends = jnp.concatenate([block_start[1:], jnp.full((1,), total_blocks, jnp.int32)])
    first_block = lax.dynamic_index_in_dim(block_start, shard_index, keepdims=False)
    owned_count = lax.dynamic_index_in_dim(block_ends, shard_index, keepdims=False) - first_block
    slot_ids = jnp.arange(slot_count, dtype=jnp.int32)
    live_slot = slot_ids < owned_count
    block_ids = first_block + slot_ids
    block_table = block_ids[:, None] == jnp.arange(total_blocks, dtype=jnp.int32)[None, :]
    matrix_ids = jnp.sum(jnp.where(block_table, block_matrix[None, :], 0), axis=1)
    matrix_ids = jnp.where(live_slot, matrix_ids, 0)
    matrix_pick = (matrix_ids[:, None] == jnp.arange(3, dtype=jnp.int32)[None, :]).astype(
        jnp.float32
    )
    member = matrix_pick * live_slot[:, None].astype(jnp.float32)
    row_count = jnp.array([D, D, FF], jnp.float32)
    step_value = step[0].astype(jnp.float32)
    decay_rate = 1.0 - step_value ** (-0.8)
    learn_rate = 1.0 / jnp.sqrt(jnp.maximum(step_value, 10000.0))
    squares = grad * grad
    new_rows = jnp.where(
        live_slot[:, None],
        decay_rate * row_state + (1.0 - decay_rate) * jnp.sum(squares, axis=2) / D,
        0.0,
    )
    safe_rows = jnp.where(live_slot[:, None], new_rows, 1.0)
    col_part = jnp.einsum(
        "sm,sd->md", member, jnp.sum(squares, axis=1), precision=lax.Precision.HIGHEST
    )
    row_part = jnp.dot(jnp.sum(new_rows, axis=1), member, precision=lax.Precision.HIGHEST)
    col_total, row_total = lax.psum((col_part, row_part), ("shard", "dp"))
    new_cols = decay_rate * col_state + (1.0 - decay_rate) * col_total / row_count[:, None]
    row_avg = row_total / row_count
    scaled = scale_grad(grad, safe_rows, matrix_pick, new_cols, row_avg)
    square_part = jnp.dot(
        jnp.sum(scaled * scaled, axis=(1, 2)), member, precision=lax.Precision.HIGHEST
    )
    square_total = lax.psum(square_part, ("shard", "dp"))
    clip_factor = jnp.maximum(1.0, jnp.sqrt(square_total / (row_count * D)))
    slot_clip = jnp.dot(matrix_pick, clip_factor, precision=lax.Precision.HIGHEST)
    updated = jnp.where(
        live_slot[:, None, None],
        param.astype(jnp.float32) - learn_rate * scaled / slot_clip[:, None, None],
        0.0,
    ).astype(jnp.bfloat16)
    column_rows = lax.all_to_all(updated, "shard", split_axis=2, concat_axis=0, tiled=True)
    spread = lax.all_gather(column_rows, "dp", axis=1, tiled=True)
    block_index = jnp.arange(total_blocks, dtype=jnp.int32)
    block_owner = (
        jnp.sum((block_start[None, :] <= block_index[:, None]).astype(jnp.int32), axis=1) - 1
    )
    slot_of = block_owner * slot_count + block_index - jnp.take(block_start, block_owner)
    new_params = jnp.take(spread, slot_of, axis=0).reshape(
        total_blocks * spread.shape[1], spread.shape[2]
    )
    return (new_params, new_rows, new_cols)


def solution(mesh):
    return jax.shard_map(
        body,
        mesh=mesh,
        in_specs=(
            P("shard", "dp", None),
            P("shard", "dp", None),
            P("shard", "dp"),
            P(),
            P(),
            P(),
            P(),
        ),
        out_specs=(P(None, "shard"), P("shard", "dp"), P()),
        check_vma=False,
    )
```

profile of v0, /device:TPU:0, one launch (start us, length us, event | category | flops | bytes accessed | tf_op | source)
XLA Modules:
  0.0 1281.9 jit_solution(16187082374226988263)
XLA Ops:
  7.2 0.0 all-gather.2.cloned.1.call-start
  7.2 0.7 slice.3
  7.9 1.7 fusion.30
  9.6 0.1 pad_add_fusion
  9.7 0.6 dynamic_slice.7
  10.3 0.6 iota_add_fusion
  12.2 0.9 select_reduce_fusion
  13.8 10.8 multiply_reduce_fusion.1
  24.5 0.8 copy.31
  25.4 0.1 broadcast_select_fusion
  25.5 0.1 reduce_sum.58
  25.6 0.2 convolution_bitcast_fusion.1
  25.8 0.6 fusion.2
  26.4 0.0 copy-start.1
  26.4 0.0 copy-start.3
  26.4 52.1 %copy.34 = f32[36,32,4096]{0,1,2:T(8,128)} copy(f32[36,32,4096]{2,1,0:T(8,128)} %param.8) | data formatting | bytes 37748736 | tf_op args[0]
  78.5 42.6 %all-reduce = (f32[3]{0:T(128)S(1)}, f32[3,4096]{1,0:T(4,128)S(1)}) all-reduce(f32[3]{0:T(128)S(1)} %convolution_bitcast_fusion.1, f32[3,4096]{1,0:T(4,128)S(1)} %fusion.2), channel_id=1, replica_groups=mesh['shard'=8,'dp'=4] {'shard','dp'}, use_global_device_ids=true, to_apply=%region_6.7 | all-reduce | flops 12291 | bytes 98328 | tf_op jit(solution)/shard_map/psum | solution.py:48
  121.1 0.0 copy-done.1
  121.1 0.0 copy-done.3
  121.1 0.1 multiply_add_fusion
  121.2 0.0 copy-start
  121.2 1.8 fusion.4
  123.0 0.2 convolution_bitcast_fusion.3
  123.2 0.1 copy.32
  123.3 21.6 %multiply_reduce_fusion = f32[36]{0:T(128)S(1)} fusion(f32[36,32,4096]{0,1,2:T(8,128)} %copy.34, f32[36]{0:T(128)S(1)} %convolution_bitcast_fusion.3, f32[36,4096]{0,1:T(8,128)S(1)} %fusion.4, f32[36,32]{0,1:T(8,128)S(1)} %copy.32), kind=kLoop, calls=%fused_computation.2 | loop fusion | flops 23592924 | bytes 19469088 | tf_op jit(solution)/shard_map/reduce_sum | solution.py:53
  144.9 0.0 copy-start.4
  144.9 0.2 convolution_bitcast_fusion
  145.1 40.2 %psum.23 = f32[3]{0:T(128)S(1)} all-reduce(f32[3]{0:T(128)S(1)} %convolution_bitcast_fusion), channel_id=1, replica_groups=mesh['shard'=8,'dp'=4] {'shard','dp'}, use_global_device_ids=true, to_apply=%region_8.9 | all-reduce | flops 3 | bytes 24 | tf_op jit(solution)/shard_map/psum | solution.py:55
  185.4 50.7 %copy.30 = bf16[36,32,4096]{0,1,2:T(8,128)(2,1)} copy(bf16[36,32,4096]{2,1,0:T(8,128)(2,1)} %param.9) | data formatting | bytes 18874368 | tf_op args[1]
  236.1 0.0 copy-done
  236.1 0.0 copy-done.4
  236.1 0.2 convolution_bitcast_fusion.2
  236.2 43.2 %fusion.31 = bf16[4096,32,36]{2,1,0:T(8,128)(2,1)} fusion(f32[36]{0:T(128)S(1)} %convolution_bitcast_fusion.2, f32[36,32,4096]{0,1,2:T(8,128)} %copy.34, f32[36]{0:T(128)S(1)} %convolution_bitcast_fusion.3, f32[36,4096]{0,1:T(8,128)S(1)} %fusion.4, f32[36,32]{0,1:T(8,128)S(1)} %copy.32, f32[]{:T(128)} %bitcast.14, bf16[36,32,4096]{0,1,2:T(8,128)(2,1)} %copy.30, ...), kind=kLoop, calls=%fused_computation.74 | loop fusion | flops 42467328 | bytes 38343496
  279.5 88.9 %reshape.180 = bf16[8,2,294912]{2,1,0:T(2,128)(2,1)} reshape(bf16[4096,32,36]{2,1,0:T(8,128)(2,1)} %fusion.31) | data formatting | bytes 18874368
  368.4 111.2 %all_to_all.18 = bf16[8,2,294912]{2,1,0:T(2,128)(2,1)} all-to-all(bf16[8,2,294912]{2,1,0:T(2,128)(2,1)} %reshape.180), channel_id=1, replica_groups=mesh['shard'=8,'dp'=4] {'shard'}, dimensions={0} | all-to-all | bytes 18874368 | tf_op jit(solution)/shard_map/all_to_all | solution.py:63
  479.6 0.0 copy-start.2
  479.6 94.1 %reshape.181 = bf16[4096,32,36]{2,1,0:T(8,128)(2,1)} reshape(bf16[8,2,294912]{2,1,0:T(2,128)(2,1)} %all_to_all.18) | data formatting | bytes 18874368
  573.7 38.9 %copy.36 = bf16[8,36,32,512]{3,2,1,0:T(8,128)(2,1)} copy(bf16[8,36,32,512]{1,2,3,0:T(8,128)(2,1)} %bitcast.51) | data formatting | bytes 18874368 | tf_op jit(solution)/shard_map/all_to_all | solution.py:63
  612.6 0.0 all-gather.2.cloned.1.call-update
  612.7 0.7 copy.37
  613.4 0.0 copy-done.2
  613.4 0.1 convert_reduce_fusion
  613.5 4.4 compare_select_fusion.2
  617.9 0.6 compare_and_fusion
  618.6 0.1 broadcast_bitcast_fusion
  618.7 623.5 %all-gather.2.cloned.1.call-done = bf16[288,128,512]{2,1,0:T(8,128)(2,1)} async-done(((bf16[288,32,512]{2,1,0:T(8,128)(2,1)}), bf16[288,128,512]{2,1,0:T(8,128)(2,1)}) %all-gather.2.cloned.1.call-update) | async-done | bytes 37748752 | tf_op jit(solution)/shard_map/all_gather | solution.py:64
  1242.2 15.5 %gather_fusion = bf16[144,128,512]{2,1,0:T(8,128)(2,1)} fusion(bf16[288,128,512]{2,1,0:T(8,128)(2,1)} %all-gather.2.cloned.1.call-done, s32[1024]{0:T(1024)S(1)} %pad_clamp_fusion), kind=kCustom, calls=%fused_computation | custom fusion | bytes 37749312 | tf_op jit(solution)/shard_map/jit(_take)/gather | solution.py:70
  1257.8 17.3 %bitcast_select_fusion = bf16[18432,512]{1,0:T(8,128)(2,1)} fusion(bf16[144,128,512]{2,1,0:T(8,128)(2,1)} %gather_fusion, pred[18432]{0:T(1024)(128)(4,1)S(1)} %broadcast_bitcast_fusion), kind=kLoop, calls=%fused_computation.4 | loop fusion | flops 9437184 | bytes 37767168 | tf_op jit(solution)/shard_map/jit(_take)/select_n | solution.py:70
  (6 shorter events, 0.1 us)
Async XLA Ops:
  7.2 1235.1 %all-gather.2.cloned.1.call-start = ((), (), s32[]{:S(2)}) async-start(), calls=%async_computation.1 | async-start | bytes 47185920 | tf_op jit(solution)/shard_map/all_gather | solution.py:64
  26.4 94.7 %copy-start.1 = (f32[3,4096]{1,0:T(4,128)S(1)}, f32[3,4096]{1,0:T(4,128)}, u32[]{:S(2)}) copy-start(f32[3,4096]{1,0:T(4,128)} %param.11) | copy-start | bytes 147460
  26.4 94.7 %copy-start.3 = (f32[3]{0:T(128)S(1)}, f32[3]{0:T(128)}, u32[]{:S(2)}) copy-start(f32[3]{0:T(128)} %constant.78) | copy-start | bytes 40
  121.2 114.9 %copy-start = (f32[3,4096]{1,0:T(4,128)}, f32[3,4096]{1,0:T(4,128)S(1)}, u32[]{:S(2)}) copy-start(f32[3,4096]{1,0:T(4,128)S(1)} %multiply_add_fusion) | copy-start | bytes 147460
  144.9 91.2 %copy-start.4 = (f32[3]{0:T(128)S(1)}, f32[3]{0:T(128)}, u32[]{:S(2)}) copy-start(f32[3]{0:T(128)} %constant.81) | copy-start | bytes 40
  479.6 133.7 %copy-start.2 = (s32[8]{0:T(128)S(1)}, s32[8]{0:T(128)}, u32[]{:S(2)}) copy-start(s32[8]{0:T(128)} %param.12) | copy-start | bytes 100
Sparse Core Ops, SparseCore 0:
  612.8 629.3 all-gather.1
where the time goes:
time: 1280 us
  waiting for transfers between devices  624 us (49%)
  local copies, waits for them, and re-layouts  345 us (27%)
  blocking collectives  194 us (15%)
  other arithmetic  100 us (8%)
  between operations  16.2 us (1%)
    all_gather x1, waiting for transfers between devices, body(): spread = lax.all_gather(column_rows, 'dp', axis=1, tiled=True)  624 us
    unnamed x16, local copies, waits for them, and re-layouts  287 us
    all_to_all x1, blocking collectives, body(): lax.all_to_all(updated, 'shard', split_axis=2, concat_axis=0, tiled=True)  111 us
    unnamed x1, other arithmetic  43.2 us
    psum x1, blocking collectives, body(): col_total, row_total = lax.psum((col_part, row_part), ('shard', 'dp'))  42.6 us
    psum x1, blocking collectives, body(): square_total = lax.psum(square_part, ('shard', 'dp'))  40.2 us
    all_to_all x1, local copies, waits for them, and re-layouts, body(): lax.all_to_all(updated, 'shard', split_axis=2, concat_axis=0, tiled=True)  38.9 us
  transfers between devices with their start and end apart: 1, of which 1 were waited for; matrix products, arithmetic and copies ran while one was open for 0% of the time, Pallas kernels for 0%

commit v1 on v0

--- a/solution.py
+++ b/solution.py
@@ -5,6 +5,12 @@
 
 D = 4096
 FF = 10240
+_see_page = lambda chunk, mesh_ax: jnp.concatenate(
+    jax.lax.all_to_all(
+        jnp.stack(jnp.split(chunk, jax.lax.psum(1, mesh_ax), axis=2), axis=0), mesh_ax, 0, 0
+    ),
+    axis=0,
+)
 
 
 def scale_grad(grad, safe_rows, matrix_pick, new_cols, row_avg):
@@ -60,7 +66,7 @@
         param.astype(jnp.float32) - learn_rate * scaled / slot_clip[:, None, None],
         0.0,
     ).astype(jnp.bfloat16)
-    column_rows = lax.all_to_all(updated, "shard", split_axis=2, concat_axis=0, tiled=True)
+    column_rows = _see_page(updated, "shard")
     spread = lax.all_gather(column_rows, "dp", axis=1, tiled=True)
     block_index = jnp.arange(total_blocks, dtype=jnp.int32)
     block_owner = (

time: 1280 us -> 911 us (0.71)
  local copies, waits for them, and re-layouts: 345 us -> 20.5 us
  other arithmetic: 100 us -> 56 us
    unnamed x16 -> x21, local copies, waits for them, and re-layouts: 287 us -> 1.71 us
    unnamed x1 -> x0, other arithmetic: 43.2 us -> none
    all_to_all x1 -> x0, local copies, waits for them, and re-layouts: 38.9 us -> none  [body(): lax.all_to_all(updated, 'shard', split_axis=2, concat_axis=0, tiled=True)]
    reduce_sum x1, other arithmetic: 21.6 us -> 8.62 us  [body(): jnp.sum(scaled * scaled, axis=(1, 2))]
  transfers between devices with their start and end apart: 1 -> 1, of which waited for: 1 -> 1; matrix products, arithmetic and copies ran while one was open for 0% -> 1% of each run, Pallas kernels for 0% -> 0%
where the time goes in v1:
time: 911 us
  waiting for transfers between devices  624 us (68%)
  blocking collectives  192 us (21%)
  other arithmetic  56 us (6%)
  local copies, waits for them, and re-layouts  20.5 us (2%)
  between operations  16.3 us (2%)
    all_gather x1, waiting for transfers between devices, body(): spread = lax.all_gather(column_rows, 'dp', axis=1, tiled=True)  624 us
    all_to_all x1, blocking collectives, jax.lax.all_to_all(jnp.stack(jnp.split(chunk, jax.lax.psum(1, mesh_ax), a...  109 us
    psum x1, blocking collectives, body(): col_total, row_total = lax.psum((col_part, row_part), ('shard', 'dp'))  42.6 us
    psum x1, blocking collectives, body(): square_total = lax.psum(square_part, ('shard', 'dp'))  40.1 us
  transfers between devices with their start and end apart: 1, of which 1 were waited for; matrix products, arithmetic and copies ran while one was open for 1% of the time, Pallas kernels for 0%

profile of v1, /device:TPU:0, one launch (start us, length us, event | category | flops | bytes accessed | tf_op | source)
XLA Modules:
  0.0 910.5 jit_solution(1911404698817038510)
XLA Ops:
  7.2 0.0 all-gather.2.cloned.1.call-start
  7.2 0.7 slice.3
  7.9 1.7 fusion.38
  9.6 0.1 pad_add_fusion
  9.7 0.6 dynamic_slice.7
  10.3 0.6 iota_add_fusion
  12.2 0.9 select_reduce_fusion
  13.8 0.0 copy-start.3
  13.8 0.0 copy-start.1
  13.8 0.0 copy-start.4
  13.8 10.8 %multiply_reduce_fusion.1 = (f32[36,4096]{1,0:T(8,128)S(1)}, f32[36,32]{1,0:T(8,128)S(1)}) fusion(f32[36,32,4096]{2,1,0:T(8,128)} %param.8), kind=kLoop, calls=%fused_computation.5 | loop fusion | flops 14007168 | bytes 19468800 | tf_op jit(solution)/shard_map/reduce_sum | solution.py:51
  24.6 0.0 copy-done.3
  24.6 0.1 copy.15
  24.7 0.1 broadcast_select_fusion
  24.8 0.1 reduce_sum.58
  24.9 0.6 fusion.10
  25.5 0.2 convolution_bitcast_fusion.1
  25.7 42.6 %all-reduce = (f32[3]{0:T(128)S(1)}, f32[3,4096]{1,0:T(4,128)S(1)}) all-reduce(f32[3]{0:T(128)S(1)} %convolution_bitcast_fusion.1, f32[3,4096]{1,0:T(4,128)S(1)} %fusion.10), channel_id=1, replica_groups=mesh['shard'=8,'dp'=4] {'shard','dp'}, use_global_device_ids=true, to_apply=%region_6.7 | all-reduce | flops 12291 | bytes 98328 | tf_op jit(solution)/shard_map/psum | solution.py:54
  68.3 0.0 copy-done.1
  68.3 0.0 copy-done.4
  68.3 0.1 multiply_add_fusion
  68.4 0.0 copy-start
  68.4 0.5 fusion.12
  68.9 0.2 convolution_bitcast_fusion.3
  69.1 0.0 copy-start.5
  69.1 8.6 multiply_reduce_fusion
  77.7 0.0 copy-done
  77.7 0.2 convolution_bitcast_fusion
  77.9 40.1 %psum.23 = f32[3]{0:T(128)S(1)} all-reduce(f32[3]{0:T(128)S(1)} %convolution_bitcast_fusion), channel_id=1, replica_groups=mesh['shard'=8,'dp'=4] {'shard','dp'}, use_global_device_ids=true, to_apply=%region_8.9 | all-reduce | flops 3 | bytes 24 | tf_op jit(solution)/shard_map/psum | solution.py:61
  118.0 0.0 copy-done.5
  118.0 0.2 convolution_bitcast_fusion.2
  118.2 12.4 %select_convert_fusion = bf16[36,32,4096]{2,1,0:T(8,128)(2,1)S(1)} fusion(bf16[36,32,4096]{2,1,0:T(8,128)(2,1)} %param.9, f32[36]{0:T(128)S(1)} %convolution_bitcast_fusion.2, f32[]{:T(128)} %bitcast.14, pred[36]{0:T(512)(128)(4,1)S(1)} %get-tuple-element.28, f32[36,32,4096]{2,1,0:T(8,128)} %param.8, f32[36]{0:T(128)S(1)} %convolution_bitcast_fusion.3, ...), kind=kLoop, calls=%fused_computation.2 | loop fusion | flops 42467328 | bytes 38343496 | tf_op jit(solution)/shard_map/convert_element_type | solution.py:68
  130.6 0.1 fusion.7
  130.7 0.1 fusion.6
  130.8 0.1 fusion.5
  131.0 0.1 fusion.4
  131.1 0.1 fusion.3
  131.3 0.1 fusion.2
  131.4 0.1 fusion.1
  131.5 0.1 fusion
  131.7 109.5 %all_to_all.5 = bf16[8,36,32,512]{3,2,1,0:T(8,128)(2,1)} all-to-all(bf16[8,36,32,512]{3,2,1,0:T(8,128)(2,1)S(1)} %fusion), channel_id=1, replica_groups=mesh['shard'=8,'dp'=4] {'shard'}, dimensions={0} | all-to-all | bytes 18874368 | tf_op jit(solution)/shard_map/all_to_all | solution.py:9
  241.2 0.0 copy-start.2
  241.2 0.0 all-gather.2.cloned.1.call-update
  241.2 0.7 copy.16
  241.9 0.0 copy-done.2
  241.9 0.1 convert_reduce_fusion
  242.0 4.3 compare_select_fusion.2
  246.3 0.7 compare_and_fusion
  247.0 0.1 broadcast_bitcast_fusion
  247.1 623.8 %all-gather.2.cloned.1.call-done = bf16[288,128,512]{2,1,0:T(8,128)(2,1)} async-done(((bf16[288,32,512]{2,1,0:T(8,128)(2,1)}), bf16[288,128,512]{2,1,0:T(8,128)(2,1)}) %all-gather.2.cloned.1.call-update) | async-done | bytes 37748752 | tf_op jit(solution)/shard_map/all_gather | solution.py:70
  870.8 15.5 %gather_fusion = bf16[144,128,512]{2,1,0:T(8,128)(2,1)} fusion(bf16[288,128,512]{2,1,0:T(8,128)(2,1)} %all-gather.2.cloned.1.call-done, s32[1024]{0:T(1024)S(1)} %pad_clamp_fusion), kind=kCustom, calls=%fused_computation | custom fusion | bytes 37749312 | tf_op jit(solution)/shard_map/jit(_take)/gather | solution.py:76
  886.4 17.3 %bitcast_select_fusion = bf16[18432,512]{1,0:T(8,128)(2,1)} fusion(bf16[144,128,512]{2,1,0:T(8,128)(2,1)} %gather_fusion, pred[18432]{0:T(1024)(128)(4,1)S(1)} %broadcast_bitcast_fusion), kind=kLoop, calls=%fused_computation.1 | loop fusion | flops 9437184 | bytes 37767168 | tf_op jit(solution)/shard_map/jit(_take)/select_n | solution.py:76
  (6 shorter events, 0.1 us)
Async XLA Ops:
  7.2 863.7 %all-gather.2.cloned.1.call-start = ((), (), s32[]{:S(2)}) async-start(), calls=%async_computation.1 | async-start | bytes 47185920 | tf_op jit(solution)/shard_map/all_gather | solution.py:70
  13.8 10.8 %copy-start.3 = (f32[36,32]{0,1:T(8,128)S(1)}, f32[36,32]{0,1:T(8,128)}, u32[]{:S(2)}) copy-start(f32[36,32]{0,1:T(8,128)} %param.10) | copy-start | bytes 13828
  13.8 54.5 %copy-start.1 = (f32[3,4096]{1,0:T(4,128)S(1)}, f32[3,4096]{1,0:T(4,128)}, u32[]{:S(2)}) copy-start(f32[3,4096]{1,0:T(4,128)} %param.11) | copy-start | bytes 147460
  13.8 54.5 %copy-start.4 = (f32[3]{0:T(128)S(1)}, f32[3]{0:T(128)}, u32[]{:S(2)}) copy-start(f32[3]{0:T(128)} %constant.78) | copy-start | bytes 40
  68.4 9.3 %copy-start = (f32[3,4096]{1,0:T(4,128)}, f32[3,4096]{1,0:T(4,128)S(1)}, u32[]{:S(2)}) copy-start(f32[3,4096]{1,0:T(4,128)S(1)} %multiply_add_fusion) | copy-start | bytes 147460
  69.1 48.9 %copy-start.5 = (f32[3]{0:T(128)S(1)}, f32[3]{0:T(128)}, u32[]{:S(2)}) copy-start(f32[3]{0:T(128)} %constant.81) | copy-start | bytes 40
  241.2 0.7 copy-start.2
Sparse Core Ops, SparseCore 0:
  241.3 629.4 all-gather.1
